TPU v7x, 128 devices: a whole 4x4x4 slice. The times are simulated.
128 devices in a mesh: dp: 8 (over x, core), mp: 16 (over y, z).
Axes of the slice: x: 4, y: 4, z: 4, core: 2. Of those that a mesh axis runs over, the one named last changes fastest.
Arguments:
- tokens: bfloat16 [256, 8192], P('dp', 'mp'), may hold values from -6 to 6
- gate_up_weight: bfloat16 [2, 8192, 15360], P(None, 'mp', 'dp'), may hold values from -0.0625 to 0.0625
- down_weight: bfloat16 [15360, 8192], P('dp', 'mp'), may hold values from -0.046875 to 0.046875
- gate_up_input_factor: bfloat16 [2, 8192, 64], P(None, 'mp'), may hold values from -0.0625 to 0.0625
- gate_up_output_factor: bfloat16 [2, 64, 15360], P(None, None, 'dp'), may hold values from -0.046875 to 0.046875
- down_input_factor: bfloat16 [15360, 64], P('dp'), may hold values from -0.046875 to 0.046875
- down_output_factor: bfloat16 [64, 8192], P(None, 'mp'), may hold values from -0.0625 to 0.0625
- cotangent: bfloat16 [256, 8192], P('dp', 'mp'), may hold values from -6 to 6
Outputs:
- output: bfloat16 [256, 8192], P('dp', 'mp')
- input_grad: bfloat16 [256, 8192], P('dp', 'mp')
- grad_gate_up_lower: float32 [2, 8192, 64], P(None, 'mp')
- gate_up_output_factor_gradient: float32 [2, 64, 15360], P(None, None, 'dp')
- down_input_factor_gradient: float32 [15360, 64], P('dp')
- down_output_factor_gradient: float32 [64, 8192], P(None, 'mp')
All inputs are finite; a program needn't handle non-finite values.
Results may differ from a plain program's by a relative error of at most 0.0065.
Values may be sent and summed in bfloat16 or wider, within the bound.
A program may use at most 64 MiB of HBM per device.

v0:
```python
import jax
import jax.numpy as jnp
from jax import lax
from jax.sharding import Mesh
from jax.sharding import PartitionSpec as P

MP = ("mp_0", "mp_1")
adapter_scale = 2.0


def sent_to_all(array, axis):
    length = lax.axis_size(axis)
    return lax.all_to_all(
        jnp.broadcast_to(array[None], (length, *array.shape)), axis, 0, 0, tiled=True
    )


def joined_along(parts, dim):
    shape = list(parts.shape[1:])
    shape[dim] *= parts.shape[0]
    return jnp.moveaxis(parts, 0, dim).reshape(shape)


def gathered_copies(array, axis, dim):
    parts = sent_to_all(array, axis)
    return joined_along(parts, dim)


def cut_along(array, dim, length):
    shape = array.shape
    parts = array.reshape(*shape[:dim], length, shape[dim] // length, *shape[dim + 1 :])
    return jnp.moveaxis(parts, dim, 0)


def piece_ends(length, count):
    hop = length // count
    if hop >= 8:
        hop -= hop % 8
    return [hop * k for k in range(1, count)]


def sum_in_order(parts, axes, turns):
    shape = [lax.axis_size(a) for a in axes]
    parts = parts.reshape(*shape, *parts.shape[1:])
    parts = parts.transpose(*turns, *range(len(axes), parts.ndim))
    parts = parts.reshape(-1, *parts.shape[len(axes) :])
    for k in turns:
        parts = lax.psum_scatter(parts, axes[k], scatter_dimension=0, tiled=True)
    return parts[0]


def sum_at_once(array, axes, dim):
    parts = cut_along(array, dim, lax.axis_size(axes))
    widest = max(range(1, max(2, parts.ndim - 1)), key=lambda d: parts.shape[d])
    count, finished = (len(axes), [])
    for first, section in enumerate(
        jnp.split(parts, piece_ends(parts.shape[widest], count), axis=widest)
    ):
        if section.size:
            turns = [(first + k) % count for k in range(count)]
            finished.append(sum_in_order(section, axes, turns))
    return jnp.concatenate(finished, axis=widest - 1)


def sum_at_owner(array, axis, dim):
    parts = cut_along(array, dim, lax.axis_size(axis))
    arrived = lax.all_to_all(parts, axis, split_axis=0, concat_axis=0, tiled=True)
    return arrived.sum(axis=0)


def over_copies(array, axis):
    return sent_to_all(array, axis).sum(axis=0)


def in_one(arrays, axis):
    ravelled, at, finished = (jnp.concatenate([a.reshape(-1) for a in arrays]), 0, [])
    so_far = over_copies(ravelled, axis)
    for a in arrays:
        finished.append(so_far[at : at + a.size].reshape(a.shape))
        at += a.size
    return tuple(finished)


def contract_trailing(left, right, matmul_precision=None):
    return lax.dot_general(
        left,
        right,
        (((1,), (1,)), ((), ())),
        preferred_element_type=jnp.float32,
        precision=matmul_precision,
    )


def contract_leading(left, right, matmul_precision=None):
    return lax.dot_general(
        left,
        right,
        (((0,), (0,)), ((), ())),
        preferred_element_type=jnp.float32,
        precision=matmul_precision,
    )


def per_device(
    tokens,
    gate_up_weight,
    down_weight,
    gate_up_input_factor,
    gate_up_output_factor,
    down_input_factor,
    down_output_factor,
    cotangent,
):
    single_float = jnp.float32
    product_precision = lax.Precision.DEFAULT
    tok_rows = tokens.shape[0]
    input_rows_full = gathered_copies(tokens, "dp", 0)
    total = input_rows_full.shape[0]
    mp_rows = total // lax.axis_size(MP)
    scale_factor = total ** (-0.5)
    mp_start = lax.axis_index(MP) * mp_rows
    dp_start = lax.axis_index("dp") * tok_rows
    low_part = jnp.einsum(
        "td,kdr->tkr", input_rows_full, gate_up_input_factor, preferred_element_type=single_float
    )
    upper_widened = gate_up_output_factor.astype(single_float)
    term = jnp.einsum(
        "td,kdf->tkf", input_rows_full, gate_up_weight, preferred_element_type=single_float
    )
    low_slab = low_part
    term = term + adapter_scale * jnp.einsum("ubw,bwa->uba", low_slab, upper_widened)
    preactivation = sum_at_once(term, MP, 0)
    gate = preactivation[:, 0]
    upper = preactivation[:, 1]
    hidden_state = (jax.nn.silu(gate) * upper).astype(jnp.bfloat16)
    hidden_state_full = gathered_copies(hidden_state, MP, 0)
    low_down_part = jnp.dot(
        hidden_state_full, down_input_factor, preferred_element_type=single_float
    )
    down_widened_rows = down_output_factor.astype(single_float)
    term = jnp.dot(hidden_state_full, down_weight, preferred_element_type=single_float)
    low_slab = low_down_part
    term = term + adapter_scale * jnp.dot(low_slab, down_widened_rows)
    output = sum_at_owner(term, "dp", 0)
    output = output.astype(jnp.bfloat16)
    cot_all = gathered_copies(cotangent, "dp", 0)
    coeff_part = contract_leading(
        low_down_part, cot_all.astype(single_float), matmul_precision=product_precision
    )
    backward_down_rows = over_copies(contract_trailing(cot_all, down_output_factor), MP).astype(
        jnp.bfloat16
    )
    hidden_state_gradient = lax.psum_scatter(
        contract_trailing(cot_all, down_weight), MP, scatter_dimension=0, tiled=True
    )
    backward_row_block = lax.dynamic_slice_in_dim(backward_down_rows, mp_start, mp_rows, 0)
    hidden_state_gradient = hidden_state_gradient + adapter_scale * contract_trailing(
        backward_row_block, down_input_factor
    )
    down_input_factor_gradient = (
        adapter_scale * scale_factor * contract_leading(hidden_state_full, backward_down_rows)
    )
    sigma = jax.nn.sigmoid(gate)
    gate_back = hidden_state_gradient * upper * sigma * (1.0 + gate * (1.0 - sigma))
    up_back = hidden_state_gradient * gate * sigma
    pre_back = jnp.stack([gate_back, up_back], axis=1).astype(jnp.bfloat16)
    back_all = gathered_copies(pre_back, MP, 0)
    upper_partial = jnp.einsum("tkr,tkf->krf", low_part, back_all.astype(single_float))
    gate_up_output_factor_gradient = adapter_scale * scale_factor * lax.psum(upper_partial, MP)
    back_low_part = jnp.einsum(
        "tkf,krf->tkr", back_all, gate_up_output_factor, preferred_element_type=single_float
    )
    back_low_sum, down_coefficient = in_one((back_low_part, coeff_part), "dp")
    down_output_factor_gradient = adapter_scale * scale_factor * down_coefficient
    backward_lower_rows = back_low_sum.astype(jnp.bfloat16)
    grad_gate_up_lower = (
        adapter_scale
        * scale_factor
        * jnp.einsum(
            "qi,qps->pis", input_rows_full, backward_lower_rows, preferred_element_type=single_float
        )
    )
    input_total_sum = sum_at_owner(
        jnp.einsum("tkf,kdf->td", back_all, gate_up_weight, preferred_element_type=single_float),
        "dp",
        0,
    )
    low_rows_back = lax.dynamic_slice_in_dim(backward_lower_rows, dp_start, tok_rows, 0)
    input_total_sum = input_total_sum + adapter_scale * jnp.einsum(
        "tkr,kdr->td", low_rows_back, gate_up_input_factor, preferred_element_type=single_float
    )
    input_grad = input_total_sum.astype(jnp.bfloat16)
    return (
        output,
        input_grad,
        grad_gate_up_lower,
        gate_up_output_factor_gradient,
        down_input_factor_gradient,
        down_output_factor_gradient,
    )


def solution(mesh):
    torus = Mesh(mesh.devices.reshape(mesh.shape["dp"], 4, 4), ("dp", "mp_0", "mp_1"))
    in_specs = (
        P("dp", MP),
        P(None, MP, "dp"),
        P("dp", MP),
        P(None, MP, None),
        P(None, None, "dp"),
        P("dp", None),
        P(None, MP),
        P("dp", MP),
    )
    out_specs = (
        P("dp", MP),
        P("dp", MP),
        P(None, MP, None),
        P(None, None, "dp"),
        P("dp", None),
        P(None, MP),
    )
    return jax.shard_map(
        per_device, mesh=torus, in_specs=in_specs, out_specs=out_specs, check_vma=False
    )
```

profile of v0, /device:TPU:0, one launch (start us, length us, event | category | flops | bytes accessed | tf_op | source)
XLA Modules:
  0.0 345.4 jit_solution(7605972328173418897)
XLA Ops:
  9.0 11.7 %all_to_all.41 = bf16[8,32,512]{2,1,0:T(8,128)(2,1)S(1)} all-to-all(bf16[8,32,512]{2,1,0:T(8,128)(2,1)S(1)} %broadcast_in_dim.12), channel_id=1, replica_groups=mesh['dp'=8,'mp_0'=4,'mp_1'=4] {'dp'}, dimensions={0} | all-to-all | bytes 524288 | tf_op jit(solution)/shard_map/all_to_all | solution.py:13
  20.7 3.4 fusion.22
  25.0 1.6 fusion.19
  26.6 1.4 copy.44
  28.1 3.0 copy.52
  31.8 9.9 %all_to_all.42 = bf16[8,32,512]{2,1,0:T(8,128)(2,1)S(1)} all-to-all(bf16[8,32,512]{2,1,0:T(8,128)(2,1)S(1)} %broadcast_in_dim.14), channel_id=1, replica_groups=mesh['dp'=8,'mp_0'=4,'mp_1'=4] {'dp'}, dimensions={0} | all-to-all | bytes 524288 | tf_op jit(solution)/shard_map/all_to_all | solution.py:13
  41.8 2.0 fusion.25
  43.8 14.1 %reduce-scatter.9.cloned.1.call-done = f32[4,8,2,1920]{3,1,2,0:T(8,128)} async-done(((f32[16,8,2,1920]{3,1,2,0:T(8,128)}), f32[4,8,2,1920]{3,1,2,0:T(8,128)}) %reduce-scatter.9.cloned.1.call-update) | async-done | bytes 491536 | tf_op jit(solution)/shard_map/reduce_scatter | solution.py:48
  59.3 5.5 %all-to-all-start.4 = ((f32[16,256,64]{1,2,0:T(8,128)}), f32[16,256,64]{1,2,0:T(8,128)}, u32[]{:S(2)}, u32[]{:S(2)}) async-start(f32[16,256,64]{1,2,0:T(8,128)} %broadcast_in_dim.15), calls=%async_computation.8 | async-start | bytes 2097152 | tf_op jit(solution)/shard_map/all_to_all | solution.py:13
  64.8 32.6 %reduce-scatter.5.cloned.1.call-done = f32[4,8,2,1920]{3,1,2,0:T(8,128)} async-done(((f32[16,8,2,1920]{3,1,2,0:T(8,128)}), f32[4,8,2,1920]{3,1,2,0:T(8,128)}) %reduce-scatter.5.cloned.1.call-update) | async-done | bytes 491536 | tf_op jit(solution)/shard_map/reduce_scatter | solution.py:48
  99.9 46.6 %all-reduce.6.cloned.1.call-done = f32[256,1920]{1,0:T(8,128)} async-done(((f32[256,1920]{1,0:T(8,128)}), f32[256,1920]{1,0:T(8,128)}) %all-reduce.6.cloned.1.call-update) | async-done | bytes 1966096
  146.5 2.1 fusion.15
  149.6 4.9 %all-to-all-start.1 = ((bf16[16,16,1920]{2,1,0:T(8,128)(2,1)}), bf16[16,16,1920]{2,1,0:T(8,128)(2,1)S(1)}, u32[]{:S(2)}, u32[]{:S(2)}) async-start(bf16[16,16,1920]{2,1,0:T(8,128)(2,1)} %broadcast_in_dim.13), calls=%async_computation.5 | async-start | bytes 1966080 | tf_op jit(solution)/shard_map/all_to_all | solution.py:13
  154.6 1.5 pad_maximum_fusion.2
  156.1 14.7 %all-to-all-done.1 = bf16[16,16,1920]{2,1,0:T(8,128)(2,1)S(1)} async-done(((bf16[16,16,1920]{2,1,0:T(8,128)(2,1)}), bf16[16,16,1920]{2,1,0:T(8,128)(2,1)S(1)}, u32[]{:S(2)}, u32[]{:S(2)}) %all-to-all-start.1) | async-done | bytes 983072 | tf_op jit(solution)/shard_map/all_to_all | solution.py:13
  170.8 2.3 broadcast_in_dim.16
  173.1 4.4 %all-to-all-start.5 = ((bf16[16,16,2,1920]{3,1,2,0:T(8,128)(2,1)}), bf16[16,16,2,1920]{3,1,2,0:T(8,128)(2,1)}, u32[]{:S(2)}, u32[]{:S(2)}) async-start(bf16[16,16,2,1920]{3,1,2,0:T(8,128)(2,1)} %broadcast_in_dim.16), calls=%async_computation.9 | async-start | bytes 3932160 | tf_op jit(solution)/shard_map/all_to_all | solution.py:13
  177.5 1.4 fusion.24
  180.0 1.5 convolution_add_fusion
  181.5 22.5 %all-to-all-done.5 = bf16[16,16,2,1920]{3,1,2,0:T(8,128)(2,1)} async-done(((bf16[16,16,2,1920]{3,1,2,0:T(8,128)(2,1)}), bf16[16,16,2,1920]{3,1,2,0:T(8,128)(2,1)}, u32[]{:S(2)}, u32[]{:S(2)}) %all-to-all-start.5) | async-done | bytes 1966112 | tf_op jit(solution)/shard_map/all_to_all | solution.py:13
  204.0 4.3 %all-to-all-start.2 = ((f32[8,32,512]{2,1,0:T(8,128)}), f32[8,32,512]{2,1,0:T(8,128)}, u32[]{:S(2)}, u32[]{:S(2)}) async-start(f32[8,32,512]{2,1,0:T(8,128)} %bitcast.110), calls=%async_computation.6 | async-start | bytes 1048576 | tf_op jit(solution)/shard_map/all_to_all | solution.py:67
  208.2 1.7 copy.45
  214.5 4.7 %fusion.3 = f32[8,32,512]{2,1,0:T(8,128)} fusion(bf16[8,32,1920,2]{2,1,0,3:T(8,128)(2,1)} %bitcast.96, bf16[2,512,1920]{2,1,0:T(8,128)(2,1)} %param.9), kind=kOutput, calls=%fused_computation.6 | convolution fusion | flops 1006632960 | bytes 6422528 | tf_op jit(solution)/shard_map/tkf,kdf->td/dot_general | solution.py:184
  219.3 4.8 %all-to-all-start.6 = ((f32[8,32,512]{2,1,0:T(8,128)}), f32[8,32,512]{2,1,0:T(8,128)}, u32[]{:S(2)}, u32[]{:S(2)}) async-start(f32[8,32,512]{2,1,0:T(8,128)} %fusion.3), calls=%async_computation.10 | async-start | bytes 1048576 | tf_op jit(solution)/shard_map/all_to_all | solution.py:67
  225.0 9.4 %all-to-all-done.6 = f32[8,32,512]{2,1,0:T(8,128)} async-done(((f32[8,32,512]{2,1,0:T(8,128)}), f32[8,32,512]{2,1,0:T(8,128)}, u32[]{:S(2)}, u32[]{:S(2)}) %all-to-all-start.6) | async-done | bytes 524320 | tf_op jit(solution)/shard_map/all_to_all | solution.py:67
  234.5 2.4 broadcast_in_dim.17
  236.9 4.5 %all-to-all-start.7 = ((f32[8,1,65536]{2,1,0:T(1,128)}), f32[8,1,65536]{2,1,0:T(1,128)}, u32[]{:S(2)}, u32[]{:S(2)}) async-start(f32[8,1,65536]{2,1,0:T(1,128)} %broadcast_in_dim.17), calls=%async_computation.11 | async-start | bytes 4194304 | tf_op jit(solution)/shard_map/all_to_all | solution.py:13
  241.6 2.9 fusion.27
  245.7 1.7 reduce_sum.36
  248.4 81.9 %all-reduce.4.cloned.1.call-done = f32[2,64,1920]{2,1,0:T(8,128)} async-done(((f32[2,64,1920]{2,1,0:T(8,128)}), f32[2,64,1920]{2,1,0:T(8,128)}) %all-reduce.4.cloned.1.call-update) | async-done | bytes 983056 | tf_op jit(solution)/shard_map/psum | solution.py:169
  330.3 2.2 broadcast_multiply_fusion
  332.5 3.2 reduce_sum.39
  (70 shorter events, 18.6 us)
Async XLA Ops:
  8.0 33.8 %copy-start = (bf16[1920,512]{1,0:T(8,128)(2,1)S(1)}, bf16[1920,512]{1,0:T(8,128)(2,1)}, u32[]{:S(2)}) copy-start(bf16[1920,512]{1,0:T(8,128)(2,1)} %param.10) | copy-start | bytes 5898244
  8.0 49.9 %reduce-scatter.9.cloned.1.call-start = ((), (), s32[]{:S(2)}) async-start(), calls=%async_computation.14 | async-start | bytes 2457600 | tf_op jit(solution)/shard_map/reduce_scatter | solution.py:48
  20.7 3.4 copy-start.6
  20.7 3.6 %copy-start.2 = (bf16[2,64,1920]{2,1,0:T(8,128)(2,1)S(1)}, bf16[2,64,1920]{2,1,0:T(8,128)(2,1)}, u32[]{:S(2)}) copy-start(bf16[2,64,1920]{2,1,0:T(8,128)(2,1)} %param.12) | copy-start | bytes 1474564
  24.3 0.7 copy-start.4
  28.0 69.3 %reduce-scatter.5.cloned.1.call-start = ((), (), s32[]{:S(2)}) async-start(), calls=%async_computation.12 | async-start | bytes 2457600 | tf_op jit(solution)/shard_map/reduce_scatter | solution.py:48
  31.1 0.8 copy-start.12
  31.1 115.4 %all-reduce.6.cloned.1.call-start = ((), (), s32[]{:S(2)}) async-start(), calls=%async_computation.17 | async-start | bytes 3932160
  43.8 14.2 %copy-start.8 = (bf16[64,512]{1,0:T(8,128)(2,1)S(1)}, bf16[64,512]{1,0:T(8,128)(2,1)}, u32[]{:S(2)}) copy-start(bf16[64,512]{1,0:T(8,128)(2,1)} %param.14) | copy-start | bytes 196612
  43.8 102.7 %reduce-scatter.11.cloned.1.call-start = ((), (), s32[]{:S(2)}) async-start(), calls=%async_computation.15 | async-start | bytes 614400 | tf_op jit(solution)/shard_map/reduce_scatter | solution.py:48
  58.2 39.2 %copy-start.13 = (u32[128]{0:T(128)S(1)}, u32[128]{0:T(128)}, u32[]{:S(2)}) copy-start(u32[128]{0:T(128)} %constant.41) | copy-start | bytes 1540
  59.2 87.3 %copy-start.9 = (bf16[1920,64]{0,1:T(8,128)(2,1)S(1)}, bf16[1920,64]{0,1:T(8,128)(2,1)}, u32[]{:S(2)}) copy-start(bf16[1920,64]{0,1:T(8,128)(2,1)} %param.13) | copy-start | bytes 737284
  59.3 39.4 %all-to-all-start.4 = ((f32[16,256,64]{1,2,0:T(8,128)}), f32[16,256,64]{1,2,0:T(8,128)}, u32[]{:S(2)}, u32[]{:S(2)}) async-start(f32[16,256,64]{1,2,0:T(8,128)} %broadcast_in_dim.15), calls=%async_computation.8 | async-start | bytes 2097152 | tf_op jit(solution)/shard_map/all_to_all | solution.py:13
  64.7 81.8 %reduce-scatter.7.cloned.1.call-start = ((), (), s32[]{:S(2)}) async-start(), calls=%async_computation.13 | async-start | bytes 614400 | tf_op jit(solution)/shard_map/reduce_scatter | solution.py:48
  99.9 49.7 %copy-start.10 = (bf16[256,64]{0,1:T(8,128)(2,1)}, bf16[256,64]{0,1:T(8,128)(2,1)S(1)}, u32[]{:S(2)}) copy-start(bf16[256,64]{0,1:T(8,128)(2,1)S(1)} %reduce_sum.37) | copy-start | bytes 98308
  149.6 21.1 %all-to-all-start.1 = ((bf16[16,16,1920]{2,1,0:T(8,128)(2,1)}), bf16[16,16,1920]{2,1,0:T(8,128)(2,1)S(1)}, u32[]{:S(2)}, u32[]{:S(2)}) async-start(bf16[16,16,1920]{2,1,0:T(8,128)(2,1)} %broadcast_in_dim.13), calls=%async_computation.5 | async-start | bytes 1966080 | tf_op jit(solution)/shard_map/all_to_all | solution.py:13
  173.1 30.9 %all-to-all-start.5 = ((bf16[16,16,2,1920]{3,1,2,0:T(8,128)(2,1)}), bf16[16,16,2,1920]{3,1,2,0:T(8,128)(2,1)}, u32[]{:S(2)}, u32[]{:S(2)}) async-start(bf16[16,16,2,1920]{3,1,2,0:T(8,128)(2,1)} %broadcast_in_dim.16), calls=%async_computation.9 | async-start | bytes 3932160 | tf_op jit(solution)/shard_map/all_to_all | solution.py:13
  204.0 15.3 %all-to-all-start.2 = ((f32[8,32,512]{2,1,0:T(8,128)}), f32[8,32,512]{2,1,0:T(8,128)}, u32[]{:S(2)}, u32[]{:S(2)}) async-start(f32[8,32,512]{2,1,0:T(8,128)} %bitcast.110), calls=%async_computation.6 | async-start | bytes 1048576 | tf_op jit(solution)/shard_map/all_to_all | solution.py:67
  208.2 3.0 copy-start.3
  210.0 1.3 copy-start.1
  219.3 15.2 %all-to-all-start.6 = ((f32[8,32,512]{2,1,0:T(8,128)}), f32[8,32,512]{2,1,0:T(8,128)}, u32[]{:S(2)}, u32[]{:S(2)}) async-start(f32[8,32,512]{2,1,0:T(8,128)} %fusion.3), calls=%async_computation.10 | async-start | bytes 1048576 | tf_op jit(solution)/shard_map/all_to_all | solution.py:67
  236.9 4.7 %copy-start.5 = (f32[256,128]{0,1:S(1)}, f32[256,128]{0,1}, u32[]{:S(2)}) copy-start(f32[256,128]{0,1} %copy-done.4) | copy-start | bytes 393220
  236.9 95.6 %all-to-all-start.7 = ((f32[8,1,65536]{2,1,0:T(1,128)}), f32[8,1,65536]{2,1,0:T(1,128)}, u32[]{:S(2)}, u32[]{:S(2)}) async-start(f32[8,1,65536]{2,1,0:T(1,128)} %broadcast_in_dim.17), calls=%async_computation.11 | async-start | bytes 4194304 | tf_op jit(solution)/shard_map/all_to_all | solution.py:13
  241.4 3.2 copy-start.11
  241.4 88.9 %all-reduce.4.cloned.1.call-start = ((), (), s32[]{:S(2)}) async-start(), calls=%async_computation.16 | async-start | bytes 1966080 | tf_op jit(solution)/shard_map/psum | solution.py:169
  332.5 4.9 %copy-start.7 = (bf16[2,512,64]{1,2,0:T(8,128)(2,1)S(1)}, bf16[2,512,64]{1,2,0:T(8,128)(2,1)}, u32[]{:S(2)}) copy-start(bf16[2,512,64]{1,2,0:T(8,128)(2,1)} %param.11) | copy-start | bytes 393220
Sparse Core Ops, SparseCore 0:
  28.2 29.7 reduce-scatter.8
  60.3 36.9 reduce-scatter.4
  99.7 21.1 reduce-scatter.10
  123.2 22.1 reduce-scatter.6
Sparse Core Ops, SparseCore 1:
  43.9 102.6 all-reduce.5
  245.8 84.5 all-reduce.3
where the time goes:
time: 347 us; the launch traced here: 345 us
  waiting for transfers between devices  222 us (64%)
  starting transfers between devices  28.8 us (8%)
  matrix products  23.7 us (7%)
  blocking collectives  21.6 us (6%)
  local copies, waits for them, and re-layouts  21.4 us (6%)
  between operations  16.2 us (5%)
  other arithmetic  12 us (3%)
    psum x1, waiting for transfers between devices, per_device(): lax.psum(upper_partial, MP)  81.9 us
    unnamed x7, waiting for transfers between devices  46.7 us
    reduce_scatter x4, waiting for transfers between devices, sum_in_order(): parts = lax.psum_scatter(parts, axes[k], scatter_dimension=0, tiled=True)  46.6 us
    all_to_all x4, waiting for transfers between devices, sent_to_all(): lax.all_to_all(jnp.broadcast_to(array[None], (length, *array.shape)), axi...  37.1 us
    all_to_all x2, blocking collectives, sent_to_all(): lax.all_to_all(jnp.broadcast_to(array[None], (length, *array.shape)), axi...  21.6 us
    all_to_all x4, starting transfers between devices, sent_to_all(): lax.all_to_all(jnp.broadcast_to(array[None], (length, *array.shape)), axi...  19.3 us
    all_to_all x2, waiting for transfers between devices, sum_at_owner(): lax.all_to_all(parts, axis, split_axis=0, concat_axis=0, tiled=True)  9.43 us
    all_to_all x2, starting transfers between devices, sum_at_owner(): lax.all_to_all(parts, axis, split_axis=0, concat_axis=0, tiled=True)  9.07 us
  transfers between devices with their start and end apart: 12, of which 7 were waited for; matrix products, arithmetic and copies ran while one was open for 10% of the time, Pallas kernels for 0%

commit v1 on v0

--- a/solution.py
+++ b/solution.py
@@ -6,6 +6,10 @@
 
 MP = ("mp_0", "mp_1")
 adapter_scale = 2.0
+
+
+def _remake_slabs(local_x, axis_key, link_axis):
+    return lax.psum(lax.psum(local_x, axis_name=axis_key), axis_name=link_axis)
 
 
 def sent_to_all(array, axis):
@@ -166,7 +170,9 @@
     pre_back = jnp.stack([gate_back, up_back], axis=1).astype(jnp.bfloat16)
     back_all = gathered_copies(pre_back, MP, 0)
     upper_partial = jnp.einsum("tkr,tkf->krf", low_part, back_all.astype(single_float))
-    gate_up_output_factor_gradient = adapter_scale * scale_factor * lax.psum(upper_partial, MP)
+    gate_up_output_factor_gradient = (
+        adapter_scale * scale_factor * _remake_slabs(upper_partial, "mp_0", "mp_1")
+    )
     back_low_part = jnp.einsum(
         "tkf,krf->tkr", back_all, gate_up_output_factor, preferred_element_type=single_float
     )

time: 347 us -> 349 us (level)
    psum x1 -> x2, waiting for transfers between devices: 81.9 us -> 83.8 us  [_remake_slabs(): return lax.psum(lax.psum(local_x, axis_name=axis_key), axis_name=link_axis)]
    unnamed x7 -> x8, waiting for transfers between devices: 46.7 us -> 46.7 us
  transfers between devices with their start and end apart: 12 -> 13, of which waited for: 7 -> 8; matrix products, arithmetic and copies ran while one was open for 10% -> 11% of each run, Pallas kernels for 0% -> 0%
where the time goes in v1:
time: 349 us; the launch traced here: 348 us
  waiting for transfers between devices  224 us (64%)
  starting transfers between devices  28.8 us (8%)
  matrix products  23.7 us (7%)
  blocking collectives  21.6 us (6%)
  local copies, waits for them, and re-layouts  21.4 us (6%)
  between operations  16.5 us (5%)
  other arithmetic  12 us (3%)
    psum x2, waiting for transfers between devices, _remake_slabs(): return lax.psum(lax.psum(local_x, axis_name=axis_key), axis_name=link_axis)  83.8 us
    unnamed x8, waiting for transfers between devices  46.7 us
    reduce_scatter x4, waiting for transfers between devices, sum_in_order(): parts = lax.psum_scatter(parts, axes[k], scatter_dimension=0, tiled=True)  46.6 us
    all_to_all x4, waiting for transfers between devices, sent_to_all(): lax.all_to_all(jnp.broadcast_to(array[None], (length, *array.shape)), axi...  37.1 us
    all_to_all x2, blocking collectives, sent_to_all(): lax.all_to_all(jnp.broadcast_to(array[None], (length, *array.shape)), axi...  21.6 us
    all_to_all x4, starting transfers between devices, sent_to_all(): lax.all_to_all(jnp.broadcast_to(array[None], (length, *array.shape)), axi...  19.3 us
    all_to_all x2, waiting for transfers between devices, sum_at_owner(): lax.all_to_all(parts, axis, split_axis=0, concat_axis=0, tiled=True)  9.43 us
    all_to_all x2, starting transfers between devices, sum_at_owner(): lax.all_to_all(parts, axis, split_axis=0, concat_axis=0, tiled=True)  9.07 us
  transfers between devices with their start and end apart: 13, of which 8 were waited for; matrix products, arithmetic and copies ran while one was open for 11% of the time, Pallas kernels for 0%

profile of v1, /device:TPU:0, one launch (start us, length us, event | category | flops | bytes accessed | tf_op | source)
XLA Modules:
  0.0 347.8 jit_solution(11447502772428553956)
XLA Ops:
  9.0 11.7 %all_to_all.41 = bf16[8,32,512]{2,1,0:T(8,128)(2,1)S(1)} all-to-all(bf16[8,32,512]{2,1,0:T(8,128)(2,1)S(1)} %broadcast_in_dim.12), channel_id=1, replica_groups=mesh['dp'=8,'mp_0'=4,'mp_1'=4] {'dp'}, dimensions={0} | all-to-all | bytes 524288 | tf_op jit(solution)/shard_map/all_to_all | solution.py:17
  20.7 3.4 fusion.22
  25.0 1.6 fusion.19
  26.6 1.4 copy.44
  28.1 3.0 copy.52
  31.8 9.9 %all_to_all.42 = bf16[8,32,512]{2,1,0:T(8,128)(2,1)S(1)} all-to-all(bf16[8,32,512]{2,1,0:T(8,128)(2,1)S(1)} %broadcast_in_dim.14), channel_id=1, replica_groups=mesh['dp'=8,'mp_0'=4,'mp_1'=4] {'dp'}, dimensions={0} | all-to-all | bytes 524288 | tf_op jit(solution)/shard_map/all_to_all | solution.py:17
  41.8 2.0 fusion.25
  43.8 14.1 %reduce-scatter.9.cloned.1.call-done = f32[4,8,2,1920]{3,1,2,0:T(8,128)} async-done(((f32[16,8,2,1920]{3,1,2,0:T(8,128)}), f32[4,8,2,1920]{3,1,2,0:T(8,128)}) %reduce-scatter.9.cloned.1.call-update) | async-done | bytes 491536 | tf_op jit(solution)/shard_map/reduce_scatter | solution.py:52
  59.3 5.5 %all-to-all-start.4 = ((f32[16,256,64]{1,2,0:T(8,128)}), f32[16,256,64]{1,2,0:T(8,128)}, u32[]{:S(2)}, u32[]{:S(2)}) async-start(f32[16,256,64]{1,2,0:T(8,128)} %broadcast_in_dim.15), calls=%async_computation.8 | async-start | bytes 2097152 | tf_op jit(solution)/shard_map/all_to_all | solution.py:17
  64.8 32.6 %reduce-scatter.5.cloned.1.call-done = f32[4,8,2,1920]{3,1,2,0:T(8,128)} async-done(((f32[16,8,2,1920]{3,1,2,0:T(8,128)}), f32[4,8,2,1920]{3,1,2,0:T(8,128)}) %reduce-scatter.5.cloned.1.call-update) | async-done | bytes 491536 | tf_op jit(solution)/shard_map/reduce_scatter | solution.py:52
  99.9 46.6 %all-reduce.9.cloned.1.call-done = f32[256,1920]{1,0:T(8,128)} async-done(((f32[256,1920]{1,0:T(8,128)}), f32[256,1920]{1,0:T(8,128)}) %all-reduce.9.cloned.1.call-update) | async-done | bytes 1966096
  146.5 2.1 fusion.15
  149.6 4.9 %all-to-all-start.1 = ((bf16[16,16,1920]{2,1,0:T(8,128)(2,1)}), bf16[16,16,1920]{2,1,0:T(8,128)(2,1)S(1)}, u32[]{:S(2)}, u32[]{:S(2)}) async-start(bf16[16,16,1920]{2,1,0:T(8,128)(2,1)} %broadcast_in_dim.13), calls=%async_computation.5 | async-start | bytes 1966080 | tf_op jit(solution)/shard_map/all_to_all | solution.py:17
  154.6 1.5 pad_maximum_fusion.2
  156.1 14.7 %all-to-all-done.1 = bf16[16,16,1920]{2,1,0:T(8,128)(2,1)S(1)} async-done(((bf16[16,16,1920]{2,1,0:T(8,128)(2,1)}), bf16[16,16,1920]{2,1,0:T(8,128)(2,1)S(1)}, u32[]{:S(2)}, u32[]{:S(2)}) %all-to-all-start.1) | async-done | bytes 983072 | tf_op jit(solution)/shard_map/all_to_all | solution.py:17
  170.8 2.3 broadcast_in_dim.16
  173.1 4.4 %all-to-all-start.5 = ((bf16[16,16,2,1920]{3,1,2,0:T(8,128)(2,1)}), bf16[16,16,2,1920]{3,1,2,0:T(8,128)(2,1)}, u32[]{:S(2)}, u32[]{:S(2)}) async-start(bf16[16,16,2,1920]{3,1,2,0:T(8,128)(2,1)} %broadcast_in_dim.16), calls=%async_computation.9 | async-start | bytes 3932160 | tf_op jit(solution)/shard_map/all_to_all | solution.py:17
  180.0 1.5 convolution_add_fusion
  181.5 22.5 %all-to-all-done.5 = bf16[16,16,2,1920]{3,1,2,0:T(8,128)(2,1)} async-done(((bf16[16,16,2,1920]{3,1,2,0:T(8,128)(2,1)}), bf16[16,16,2,1920]{3,1,2,0:T(8,128)(2,1)}, u32[]{:S(2)}, u32[]{:S(2)}) %all-to-all-start.5) | async-done | bytes 1966112 | tf_op jit(solution)/shard_map/all_to_all | solution.py:17
  204.0 4.3 %all-to-all-start.2 = ((f32[8,32,512]{2,1,0:T(8,128)}), f32[8,32,512]{2,1,0:T(8,128)}, u32[]{:S(2)}, u32[]{:S(2)}) async-start(f32[8,32,512]{2,1,0:T(8,128)} %bitcast.110), calls=%async_computation.6 | async-start | bytes 1048576 | tf_op jit(solution)/shard_map/all_to_all | solution.py:71
  208.2 1.7 copy.45
  214.5 4.7 %fusion.3 = f32[8,32,512]{2,1,0:T(8,128)} fusion(bf16[8,32,1920,2]{2,1,0,3:T(8,128)(2,1)} %bitcast.96, bf16[2,512,1920]{2,1,0:T(8,128)(2,1)} %param.9), kind=kOutput, calls=%fused_computation.6 | convolution fusion | flops 1006632960 | bytes 6422528 | tf_op jit(solution)/shard_map/tkf,kdf->td/dot_general | solution.py:190
  219.3 4.8 %all-to-all-start.6 = ((f32[8,32,512]{2,1,0:T(8,128)}), f32[8,32,512]{2,1,0:T(8,128)}, u32[]{:S(2)}, u32[]{:S(2)}) async-start(f32[8,32,512]{2,1,0:T(8,128)} %fusion.3), calls=%async_computation.10 | async-start | bytes 1048576 | tf_op jit(solution)/shard_map/all_to_all | solution.py:71
  225.0 9.4 %all-to-all-done.6 = f32[8,32,512]{2,1,0:T(8,128)} async-done(((f32[8,32,512]{2,1,0:T(8,128)}), f32[8,32,512]{2,1,0:T(8,128)}, u32[]{:S(2)}, u32[]{:S(2)}) %all-to-all-start.6) | async-done | bytes 524320 | tf_op jit(solution)/shard_map/all_to_all | solution.py:71
  234.5 2.4 broadcast_in_dim.17
  236.9 4.5 %all-to-all-start.7 = ((f32[8,1,65536]{2,1,0:T(1,128)}), f32[8,1,65536]{2,1,0:T(1,128)}, u32[]{:S(2)}, u32[]{:S(2)}) async-start(f32[8,1,65536]{2,1,0:T(1,128)} %broadcast_in_dim.17), calls=%async_computation.11 | async-start | bytes 4194304 | tf_op jit(solution)/shard_map/all_to_all | solution.py:17
  241.4 2.9 fusion.27
  245.7 1.7 reduce_sum.36
  248.5 40.5 %all-reduce.5.cloned.1.call-done = f32[2,64,1920]{2,1,0:T(8,128)} async-done(((f32[2,64,1920]{2,1,0:T(8,128)}), f32[2,64,1920]{2,1,0:T(8,128)}) %all-reduce.5.cloned.1.call-update) | async-done | bytes 983056 | tf_op jit(solution)/shard_map/psum | solution.py:12
  289.0 3.2 reduce_sum.39
  294.7 43.4 %all-reduce.7.cloned.1.call-done = f32[2,64,1920]{2,1,0:T(8,128)} async-done(((f32[2,64,1920]{2,1,0:T(8,128)}), f32[2,64,1920]{2,1,0:T(8,128)}) %all-reduce.7.cloned.1.call-update) | async-done | bytes 983056 | tf_op jit(solution)/shard_map/psum | solution.py:12
  338.1 2.2 broadcast_multiply_fusion
  (73 shorter events, 20.1 us)
Async XLA Ops:
  8.0 33.8 %copy-start = (bf16[1920,512]{1,0:T(8,128)(2,1)S(1)}, bf16[1920,512]{1,0:T(8,128)(2,1)}, u32[]{:S(2)}) copy-start(bf16[1920,512]{1,0:T(8,128)(2,1)} %param.10) | copy-start | bytes 5898244
  8.0 49.9 %reduce-scatter.9.cloned.1.call-start = ((), (), s32[]{:S(2)}) async-start(), calls=%async_computation.14 | async-start | bytes 2457600 | tf_op jit(solution)/shard_map/reduce_scatter | solution.py:52
  20.7 3.4 copy-start.6
  20.7 3.6 %copy-start.2 = (bf16[2,64,1920]{2,1,0:T(8,128)(2,1)S(1)}, bf16[2,64,1920]{2,1,0:T(8,128)(2,1)}, u32[]{:S(2)}) copy-start(bf16[2,64,1920]{2,1,0:T(8,128)(2,1)} %param.12) | copy-start | bytes 1474564
  24.3 0.7 copy-start.4
  28.0 69.3 %reduce-scatter.5.cloned.1.call-start = ((), (), s32[]{:S(2)}) async-start(), calls=%async_computation.12 | async-start | bytes 2457600 | tf_op jit(solution)/shard_map/reduce_scatter | solution.py:52
  31.1 0.8 copy-start.12
  31.1 115.4 %all-reduce.9.cloned.1.call-start = ((), (), s32[]{:S(2)}) async-start(), calls=%async_computation.18 | async-start | bytes 3932160
  43.8 14.2 %copy-start.8 = (bf16[64,512]{1,0:T(8,128)(2,1)S(1)}, bf16[64,512]{1,0:T(8,128)(2,1)}, u32[]{:S(2)}) copy-start(bf16[64,512]{1,0:T(8,128)(2,1)} %param.14) | copy-start | bytes 196612
  43.8 102.7 %reduce-scatter.11.cloned.1.call-start = ((), (), s32[]{:S(2)}) async-start(), calls=%async_computation.15 | async-start | bytes 614400 | tf_op jit(solution)/shard_map/reduce_scatter | solution.py:52
  58.2 39.2 %copy-start.13 = (u32[128]{0:T(128)S(1)}, u32[128]{0:T(128)}, u32[]{:S(2)}) copy-start(u32[128]{0:T(128)} %constant.41) | copy-start | bytes 1540
  59.2 87.3 %copy-start.9 = (bf16[1920,64]{0,1:T(8,128)(2,1)S(1)}, bf16[1920,64]{0,1:T(8,128)(2,1)}, u32[]{:S(2)}) copy-start(bf16[1920,64]{0,1:T(8,128)(2,1)} %param.13) | copy-start | bytes 737284
  59.3 39.4 %all-to-all-start.4 = ((f32[16,256,64]{1,2,0:T(8,128)}), f32[16,256,64]{1,2,0:T(8,128)}, u32[]{:S(2)}, u32[]{:S(2)}) async-start(f32[16,256,64]{1,2,0:T(8,128)} %broadcast_in_dim.15), calls=%async_computation.8 | async-start | bytes 2097152 | tf_op jit(solution)/shard_map/all_to_all | solution.py:17
  64.7 81.8 %reduce-scatter.7.cloned.1.call-start = ((), (), s32[]{:S(2)}) async-start(), calls=%async_computation.13 | async-start | bytes 614400 | tf_op jit(solution)/shard_map/reduce_scatter | solution.py:52
  99.9 49.7 %copy-start.10 = (bf16[256,64]{0,1:T(8,128)(2,1)}, bf16[256,64]{0,1:T(8,128)(2,1)S(1)}, u32[]{:S(2)}) copy-start(bf16[256,64]{0,1:T(8,128)(2,1)S(1)} %reduce_sum.37) | copy-start | bytes 98308
  149.6 21.1 %all-to-all-start.1 = ((bf16[16,16,1920]{2,1,0:T(8,128)(2,1)}), bf16[16,16,1920]{2,1,0:T(8,128)(2,1)S(1)}, u32[]{:S(2)}, u32[]{:S(2)}) async-start(bf16[16,16,1920]{2,1,0:T(8,128)(2,1)} %broadcast_in_dim.13), calls=%async_computation.5 | async-start | bytes 1966080 | tf_op jit(solution)/shard_map/all_to_all | solution.py:17
  173.1 30.9 %all-to-all-start.5 = ((bf16[16,16,2,1920]{3,1,2,0:T(8,128)(2,1)}), bf16[16,16,2,1920]{3,1,2,0:T(8,128)(2,1)}, u32[]{:S(2)}, u32[]{:S(2)}) async-start(bf16[16,16,2,1920]{3,1,2,0:T(8,128)(2,1)} %broadcast_in_dim.16), calls=%async_computation.9 | async-start | bytes 3932160 | tf_op jit(solution)/shard_map/all_to_all | solution.py:17
  204.0 15.3 %all-to-all-start.2 = ((f32[8,32,512]{2,1,0:T(8,128)}), f32[8,32,512]{2,1,0:T(8,128)}, u32[]{:S(2)}, u32[]{:S(2)}) async-start(f32[8,32,512]{2,1,0:T(8,128)} %bitcast.110), calls=%async_computation.6 | async-start | bytes 1048576 | tf_op jit(solution)/shard_map/all_to_all | solution.py:71
  208.2 3.0 copy-start.3
  210.0 1.3 copy-start.1
  219.3 15.2 %all-to-all-start.6 = ((f32[8,32,512]{2,1,0:T(8,128)}), f32[8,32,512]{2,1,0:T(8,128)}, u32[]{:S(2)}, u32[]{:S(2)}) async-start(f32[8,32,512]{2,1,0:T(8,128)} %fusion.3), calls=%async_computation.10 | async-start | bytes 1048576 | tf_op jit(solution)/shard_map/all_to_all | solution.py:71
  236.9 4.5 %copy-start.5 = (f32[256,128]{0,1:S(1)}, f32[256,128]{0,1}, u32[]{:S(2)}) copy-start(f32[256,128]{0,1} %copy-done.4) | copy-start | bytes 393220
  236.9 52.1 %all-to-all-start.7 = ((f32[8,1,65536]{2,1,0:T(1,128)}), f32[8,1,65536]{2,1,0:T(1,128)}, u32[]{:S(2)}, u32[]{:S(2)}) async-start(f32[8,1,65536]{2,1,0:T(1,128)} %broadcast_in_dim.17), calls=%async_computation.11 | async-start | bytes 4194304 | tf_op jit(solution)/shard_map/all_to_all | solution.py:17
  241.4 3.2 copy-start.11
  241.4 47.6 %all-reduce.5.cloned.1.call-start = ((), (), s32[]{:S(2)}) async-start(), calls=%async_computation.16 | async-start | bytes 1966080 | tf_op jit(solution)/shard_map/psum | solution.py:12
  244.4 93.7 %all-reduce.7.cloned.1.call-start = ((), (), s32[]{:S(2)}) async-start(), calls=%async_computation.17 | async-start | bytes 1966080 | tf_op jit(solution)/shard_map/psum | solution.py:12
  288.9 4.0 %copy-start.7 = (bf16[2,512,64]{1,2,0:T(8,128)(2,1)S(1)}, bf16[2,512,64]{1,2,0:T(8,128)(2,1)}, u32[]{:S(2)}) copy-start(bf16[2,512,64]{1,2,0:T(8,128)(2,1)} %param.11) | copy-start | bytes 393220
Sparse Core Ops, SparseCore 0:
  28.2 29.7 reduce-scatter.8
  60.3 36.9 reduce-scatter.4
  99.7 21.1 reduce-scatter.10
  123.2 22.1 reduce-scatter.6
  244.8 44.0 all-reduce.4
  291.2 46.8 all-reduce.6
Sparse Core Ops, SparseCore 1:
  43.9 102.6 all-reduce.8
